TPU v7x, 32 devices: a whole 2x2x4 slice. The times are simulated.
32 devices in a mesh: span: 4 (over y, x), heads: 8 (over z, core).
Axes of the slice: x: 2, y: 2, z: 4, core: 2. Of those that a mesh axis runs over, the one named last changes fastest.
Arguments:
- latents: bfloat16 [4, 6144, 512], P(None, ('span', 'heads')), may hold values from -6 to 6
- rotary_rows: bfloat16 [4, 6144, 64], P(None, ('span', 'heads')), may hold values from -6 to 6
- latent_gain: float32 [512], replicated, may hold values from 0.25 to 1.75
- key_up: bfloat16 [512, 16, 128], P(None, 'heads'), may hold values from -0.25 to 0.25
- value_up: bfloat16 [512, 16, 128], P(None, 'heads'), may hold values from -0.25 to 0.25
Outputs:
- stored_keys: bfloat16 [4, 6144, 16, 192], P('span', None, 'heads')
- stored_values: bfloat16 [4, 6144, 16, 128], P('span', None, 'heads')
All inputs are finite; a program needn't handle non-finite values.
Results may differ from a plain program's by a relative error of at most 0.001.
Values may be sent and summed in bfloat16 or wider, within the bound.
A program may use at most 128 MiB of HBM per device.

v0:
```python
import jax
import jax.numpy as jnp
from jax import lax
from jax.sharding import PartitionSpec as P


def expand_rows(rows, rotary, key_up, value_up):
    wide_keys = jnp.einsum(
        "btr,rhk->bthk", rows, key_up, preferred_element_type=jnp.float32
    ).astype(jnp.bfloat16)
    shared = jnp.broadcast_to(rotary[:, :, None], wide_keys.shape[:3] + rotary.shape[2:])
    wide_values = jnp.einsum(
        "btr,rhk->bthk", rows, value_up, preferred_element_type=jnp.float32
    ).astype(jnp.bfloat16)
    return (jnp.concatenate([wide_keys, shared], axis=-1), wide_values)


def root_norm(vectors, row_gain):
    return (
        vectors * lax.rsqrt(jnp.mean(vectors * vectors, axis=-1, keepdims=True) + 1e-06) * row_gain
    )


def per_device(latents, rotary_rows, latent_gain, key_up, value_up):
    rows_ready = root_norm(latents.astype(jnp.float32), latent_gain).astype(jnp.bfloat16)
    rows_moved, rotary_moved = (
        lax.all_to_all(rows_ready, "span", split_axis=0, concat_axis=1, tiled=True),
        lax.all_to_all(rotary_rows, "span", split_axis=0, concat_axis=1, tiled=True),
    )
    rows_cut = rows_moved.reshape(
        rows_moved.shape[0], lax.axis_size("span"), -1, rows_moved.shape[2]
    )
    rotary_cut = rotary_moved.reshape(
        rotary_moved.shape[0], lax.axis_size("span"), -1, rotary_moved.shape[2]
    )
    rows_joined, rotary_joined = (
        lax.all_gather(rows_cut, "heads", axis=2, tiled=True),
        lax.all_gather(rotary_cut, "heads", axis=2, tiled=True),
    )
    rows_whole = rows_joined.reshape(rows_joined.shape[0], -1, rows_joined.shape[3])
    rotary_whole = rotary_joined.reshape(rotary_joined.shape[0], -1, rotary_joined.shape[3])
    stored_keys, stored_values = expand_rows(rows_whole, rotary_whole, key_up, value_up)
    return (stored_keys, stored_values)


def solution(mesh):
    in_specs = (
        P(None, ("span", "heads"), None),
        P(None, ("span", "heads"), None),
        P(),
        P(None, "heads", None),
        P(None, "heads", None),
    )
    out_specs = (P("span", None, "heads", None), P("span", None, "heads", None))
    return jax.shard_map(
        per_device, mesh=mesh, in_specs=in_specs, out_specs=out_specs, check_vma=False
    )
```

profile of v0, /device:TPU:0, one launch (start us, length us, event | category | flops | bytes accessed | tf_op | source)
XLA Modules:
  0.0 149.0 jit_solution(12033314378571793330)
XLA Ops:
  7.2 0.0 copy-start
  7.2 0.0 copy-start.2
  7.2 0.0 all-gather.4.cloned.1.call-start
  7.2 1.4 fusion.1
  8.7 1.4 fusion.3
  10.1 16.4 %all_to_all.8 = bf16[4,192,512]{2,1,0:T(8,128)(2,1)} all-to-all(bf16[4,192,512]{2,1,0:T(8,128)(2,1)S(1)} %fusion.3), channel_id=1, replica_groups=mesh['span'=4,'heads'=8] {'span'}, dimensions={0} | all-to-all | bytes 1572864 | tf_op jit(solution)/shard_map/all_to_all | solution.py:27
  26.5 0.0 all-gather.4.cloned.1.call-update
  26.5 3.3 %all-to-all-start.1 = ((bf16[4,192,64]{1,2,0:T(8,128)(2,1)}), bf16[4,192,64]{1,2,0:T(8,128)(2,1)S(1)}, u32[]{:S(2)}, u32[]{:S(2)}) async-start(bf16[4,192,64]{1,2,0:T(8,128)(2,1)} %param.6), calls=%async_computation.1 | async-start | bytes 262144 | tf_op jit(solution)/shard_map/all_to_all | solution.py:28
  29.9 0.0 copy-done.2
  29.9 0.2 copy.19
  30.1 4.8 %all-to-all-done.1 = bf16[4,192,64]{1,2,0:T(8,128)(2,1)S(1)} async-done(((bf16[4,192,64]{1,2,0:T(8,128)(2,1)}), bf16[4,192,64]{1,2,0:T(8,128)(2,1)S(1)}, u32[]{:S(2)}, u32[]{:S(2)}) %all-to-all-start.1) | async-done | bytes 98336 | tf_op jit(solution)/shard_map/all_to_all | solution.py:28
  34.9 0.2 copy.20
  35.0 31.3 %all-gather.1 = bf16[4,1536,64]{2,0,1:T(4,128)(2,1)S(1)} all-gather(bf16[4,192,64]{2,0,1:T(4,128)(2,1)S(1)} %copy.20), channel_id=3, replica_groups=mesh['span'=4,'heads'=8] {'heads'}, dimensions={1}, use_global_device_ids=true | all-gather | bytes 884736 | tf_op jit(solution)/shard_map/all_gather | solution.py:38
  66.4 1.2 copy.21
  67.5 0.1 copy.24
  67.7 35.9 %all-gather.4.cloned.1.call-done = bf16[4,1536,512]{2,1,0:T(8,128)(2,1)} async-done(((bf16[4,192,512]{2,1,0:T(8,128)(2,1)}), bf16[4,1536,512]{2,1,0:T(8,128)(2,1)}) %all-gather.4.cloned.1.call-update) | async-done | bytes 6291472 | tf_op jit(solution)/shard_map/all_gather | solution.py:37
  103.6 4.6 %fusion.5 = f32[6144,256]{0,1:S(1)} fusion(bf16[6144,512]{1,0:T(8,128)(2,1)} %bitcast.17, bf16[512,256]{0,1:T(8,128)(2,1)S(1)} %bitcast.21), kind=kOutput, calls=%fused_computation.11 | convolution fusion | flops 1610612736 | bytes 12845056
  108.2 0.0 copy-start.1
  108.2 0.4 convert_bitcast_fusion
  108.6 0.0 copy-done
  108.6 2.3 %copy-done.1 = bf16[4,1536,512]{2,1,0:T(8,128)(2,1)S(1)} copy-done((bf16[4,1536,512]{2,1,0:T(8,128)(2,1)S(1)}, bf16[4,1536,512]{2,1,0:T(8,128)(2,1)}, u32[]{:S(2)}) %copy-start.1) | copy-done | bytes 6291480
  111.0 1.8 %fusion = bf16[1,6144,2,128]{3,1,2,0:T(8,128)(2,1)S(1)} fusion(bf16[6144,512,1]{1,0,2:T(8,128)(2,1)S(1)} %bitcast.18, bf16[512,2,128]{2,1,0:T(2,128)(2,1)S(1)} %copy-done), kind=kOutput, calls=%fused_computation.1 | convolution fusion | flops 1612185600 | bytes 9699328 | tf_op jit(solution)/shard_map/btr,rhk->bthk/dot_general | solution.py:12
  112.8 26.8 %copy.23 = bf16[1,6144,2,128]{3,2,1,0:T(2,128)(2,1)} copy(bf16[1,6144,2,128]{3,1,2,0:T(8,128)(2,1)S(1)} %fusion) | data formatting | bytes 6291456
  139.5 0.1 broadcast_in_dim.10
  139.7 2.5 %pad_maximum_fusion = bf16[1,6144,2,192]{1,3,2,0:T(8,128)(2,1)} fusion(bf16[1,6144,2,64]{1,3,2,0:T(8,128)(2,1)S(1)} %broadcast_in_dim.10, bf16[1,6144,2,128]{1,3,2,0:T(8,128)(2,1)S(1)} %convert_bitcast_fusion), kind=kLoop, calls=%fused_computation.2 | loop fusion | flops 9437184 | bytes 9437184 | tf_op jit(solution)/shard_map/concatenate | solution.py:15
  (1 shorter events, 0.0 us)
Async XLA Ops:
  7.2 101.5 %copy-start = (bf16[512,2,128]{2,1,0:T(2,128)(2,1)S(1)}, bf16[512,2,128]{2,1,0:T(2,128)(2,1)}, u32[]{:S(2)}) copy-start(bf16[512,2,128]{2,1,0:T(2,128)(2,1)} %param.9) | copy-start | bytes 786436
  7.2 22.7 %copy-start.2 = (bf16[512,2,128]{2,1,0:T(2,128)(2,1)S(1)}, bf16[512,2,128]{2,1,0:T(2,128)(2,1)}, u32[]{:S(2)}) copy-start(bf16[512,2,128]{2,1,0:T(2,128)(2,1)} %param.8) | copy-start | bytes 786436
  7.2 96.4 %all-gather.4.cloned.1.call-start = ((), (), s32[]{:S(2)}) async-start(), calls=%async_computation.2 | async-start | bytes 7077888 | tf_op jit(solution)/shard_map/all_gather | solution.py:37
  26.5 8.3 %all-to-all-start.1 = ((bf16[4,192,64]{1,2,0:T(8,128)(2,1)}), bf16[4,192,64]{1,2,0:T(8,128)(2,1)S(1)}, u32[]{:S(2)}, u32[]{:S(2)}) async-start(bf16[4,192,64]{1,2,0:T(8,128)(2,1)} %param.6), calls=%async_computation.1 | async-start | bytes 262144 | tf_op jit(solution)/shard_map/all_to_all | solution.py:28
  108.2 2.8 %copy-start.1 = (bf16[4,1536,512]{2,1,0:T(8,128)(2,1)S(1)}, bf16[4,1536,512]{2,1,0:T(8,128)(2,1)}, u32[]{:S(2)}) copy-start(bf16[4,1536,512]{2,1,0:T(8,128)(2,1)} %all-gather.4.cloned.1.call-done) | copy-start | bytes 18874372
Sparse Core Ops, SparseCore 0:
  26.6 76.8 all-gather.3
where the time goes:
time: 149 us
  blocking collectives  47.8 us (32%)
  waiting for transfers between devices  40.7 us (27%)
  local copies, waits for them, and re-layouts  30.9 us (21%)
  between operations  14.2 us (10%)
  matrix products  6.4 us (4%)
  other arithmetic  5.74 us (4%)
  starting transfers between devices  3.38 us (2%)
    all_gather x1, waiting for transfers between devices, per_device(): lax.all_gather(rows_cut, 'heads', axis=2, tiled=True)  35.9 us
    all_gather x1, blocking collectives, per_device(): lax.all_gather(rotary_cut, 'heads', axis=2, tiled=True)  31.3 us
    unnamed x9, local copies, waits for them, and re-layouts  29.4 us
    all_to_all x1, blocking collectives, per_device(): lax.all_to_all(rows_ready, 'span', split_axis=0, concat_axis=1, tiled=True)  16.4 us
    all_to_all x1, waiting for transfers between devices, per_device(): lax.all_to_all(rotary_rows, 'span', split_axis=0, concat_axis=1, tiled=True)  4.81 us
    unnamed x1, matrix products  4.61 us
    all_to_all x1, starting transfers between devices, per_device(): lax.all_to_all(rotary_rows, 'span', split_axis=0, concat_axis=1, tiled=True)  3.34 us
  transfers between devices with their start and end apart: 2, of which 2 were waited for; matrix products, arithmetic and copies ran while one was open for 1% of the time, Pallas kernels for 0%

commit v1 on v0

--- a/solution.py
+++ b/solution.py
@@ -25,7 +25,12 @@
     rows_ready = root_norm(latents.astype(jnp.float32), latent_gain).astype(jnp.bfloat16)
     rows_moved, rotary_moved = (
         lax.all_to_all(rows_ready, "span", split_axis=0, concat_axis=1, tiled=True),
-        lax.all_to_all(rotary_rows, "span", split_axis=0, concat_axis=1, tiled=True),
+        jnp.concatenate(
+            lax.all_to_all(
+                jnp.stack(jnp.split(rotary_rows, lax.axis_size("span"), axis=0)), "span", 0, 0
+            ),
+            axis=1,
+        ),
     )
     rows_cut = rows_moved.reshape(
         rows_moved.shape[0], lax.axis_size("span"), -1, rows_moved.shape[2]

time: 149 us -> 149 us (level)
    unnamed x9 -> x11, local copies, waits for them, and re-layouts: 29.4 us -> 29.4 us
  transfers between devices with their start and end apart: 2 -> 2, of which waited for: 2 -> 2; matrix products, arithmetic and copies ran while one was open for 1% -> 2% of each run, Pallas kernels for 0% -> 0%
where the time goes in v1:
time: 149 us
  blocking collectives  47.8 us (32%)
  waiting for transfers between devices  40 us (27%)
  local copies, waits for them, and re-layouts  30.9 us (21%)
  between operations  14.2 us (10%)
  other arithmetic  6.43 us (4%)
  matrix products  6.41 us (4%)
  starting transfers between devices  3.36 us (2%)
    all_gather x1, waiting for transfers between devices, per_device(): lax.all_gather(rows_cut, 'heads', axis=2, tiled=True)  35.2 us
    all_gather x1, blocking collectives, per_device(): lax.all_gather(rotary_cut, 'heads', axis=2, tiled=True)  31.3 us
    unnamed x11, local copies, waits for them, and re-layouts  29.4 us
    all_to_all x1, blocking collectives, per_device(): lax.all_to_all(rows_ready, 'span', split_axis=0, concat_axis=1, tiled=True)  16.4 us
    all_to_all x1, waiting for transfers between devices, per_device(): lax.all_to_all(jnp.stack(jnp.split(rotary_rows, lax.axis_size('span'), ax...  4.81 us
    unnamed x1, matrix products  4.61 us
    all_to_all x1, starting transfers between devices, per_device(): lax.all_to_all(jnp.stack(jnp.split(rotary_rows, lax.axis_size('span'), ax...  3.33 us
  transfers between devices with their start and end apart: 2, of which 2 were waited for; matrix products, arithmetic and copies ran while one was open for 2% of the time, Pallas kernels for 0%

profile of v1, /device:TPU:0, one launch (start us, length us, event | category | flops | bytes accessed | tf_op | source)
XLA Modules:
  0.0 149.0 jit_solution(16935356483599078159)
XLA Ops:
  7.2 0.0 copy-start
  7.2 0.0 copy-start.3
  7.2 0.0 copy-start.2
  7.2 0.0 all-gather.4.cloned.1.call-start
  7.2 1.4 fusion.1
  8.7 1.4 fusion.3
  10.1 16.4 %all_to_all.14 = bf16[4,192,512]{2,1,0:T(8,128)(2,1)} all-to-all(bf16[4,192,512]{2,1,0:T(8,128)(2,1)S(1)} %fusion.3), channel_id=1, replica_groups=mesh['span'=4,'heads'=8] {'span'}, dimensions={0} | all-to-all | bytes 1572864 | tf_op jit(solution)/shard_map/all_to_all | solution.py:27
  26.5 0.0 all-gather.4.cloned.1.call-update
  26.5 0.0 copy-done.3
  26.6 0.7 pad_maximum_fusion.1
  27.3 3.3 %all-to-all-start.1 = ((bf16[4,1,192,64]{2,3,1,0:T(8,128)(2,1)}), bf16[4,1,192,64]{2,3,1,0:T(8,128)(2,1)S(1)}, u32[]{:S(2)}, u32[]{:S(2)}) async-start(bf16[4,1,192,64]{2,3,1,0:T(8,128)(2,1)} %pad_maximum_fusion.1), calls=%async_computation.1 | async-start | bytes 262144 | tf_op jit(solution)/shard_map/all_to_all | solution.py:29
  30.6 0.0 copy-done.2
  30.6 0.2 copy.22
  30.8 4.8 %all-to-all-done.1 = bf16[4,1,192,64]{2,3,1,0:T(8,128)(2,1)S(1)} async-done(((bf16[4,1,192,64]{2,3,1,0:T(8,128)(2,1)}), bf16[4,1,192,64]{2,3,1,0:T(8,128)(2,1)S(1)}, u32[]{:S(2)}, u32[]{:S(2)}) %all-to-all-start.1) | async-done | bytes 98336 | tf_op jit(solution)/shard_map/all_to_all | solution.py:29
  35.6 0.2 copy.23
  35.7 31.3 %all-gather.1 = bf16[4,1,1536,64]{3,0,1,2:T(4,128)(2,1)S(1)} all-gather(bf16[4,1,192,64]{3,0,1,2:T(4,128)(2,1)S(1)} %copy.23), channel_id=3, replica_groups=mesh['span'=4,'heads'=8] {'heads'}, dimensions={2}, use_global_device_ids=true | all-gather | bytes 884736 | tf_op jit(solution)/shard_map/all_gather | solution.py:43
  67.1 1.2 copy.24
  68.3 0.1 copy.27
  68.4 35.2 %all-gather.4.cloned.1.call-done = bf16[4,1536,512]{2,1,0:T(8,128)(2,1)} async-done(((bf16[4,192,512]{2,1,0:T(8,128)(2,1)}), bf16[4,1536,512]{2,1,0:T(8,128)(2,1)}) %all-gather.4.cloned.1.call-update) | async-done | bytes 6291472 | tf_op jit(solution)/shard_map/all_gather | solution.py:42
  103.6 4.6 %fusion.5 = f32[6144,256]{0,1:S(1)} fusion(bf16[6144,512]{1,0:T(8,128)(2,1)} %bitcast.26, bf16[512,256]{0,1:T(8,128)(2,1)S(1)} %bitcast.30), kind=kOutput, calls=%fused_computation.16 | convolution fusion | flops 1610612736 | bytes 12845056
  108.2 0.0 copy-start.1
  108.2 0.4 convert_bitcast_fusion
  108.6 0.0 copy-done
  108.6 2.3 %copy-done.1 = bf16[4,1536,512]{2,1,0:T(8,128)(2,1)S(1)} copy-done((bf16[4,1536,512]{2,1,0:T(8,128)(2,1)S(1)}, bf16[4,1536,512]{2,1,0:T(8,128)(2,1)}, u32[]{:S(2)}) %copy-start.1) | copy-done | bytes 6291480
  111.0 1.8 %fusion = bf16[1,6144,2,128]{3,1,2,0:T(8,128)(2,1)S(1)} fusion(bf16[6144,512,1]{1,0,2:T(8,128)(2,1)S(1)} %bitcast.27, bf16[512,2,128]{2,1,0:T(2,128)(2,1)S(1)} %copy-done), kind=kOutput, calls=%fused_computation.1 | convolution fusion | flops 1612185600 | bytes 9699328 | tf_op jit(solution)/shard_map/btr,rhk->bthk/dot_general | solution.py:12
  112.8 26.8 %copy.26 = bf16[1,6144,2,128]{3,2,1,0:T(2,128)(2,1)} copy(bf16[1,6144,2,128]{3,1,2,0:T(8,128)(2,1)S(1)} %fusion) | data formatting | bytes 6291456
  139.5 0.1 broadcast_in_dim.10
  139.7 2.5 %pad_maximum_fusion = bf16[1,6144,2,192]{1,3,2,0:T(8,128)(2,1)} fusion(bf16[1,6144,2,64]{1,3,2,0:T(8,128)(2,1)S(1)} %broadcast_in_dim.10, bf16[1,6144,2,128]{1,3,2,0:T(8,128)(2,1)S(1)} %convert_bitcast_fusion), kind=kLoop, calls=%fused_computation.2 | loop fusion | flops 9437184 | bytes 9437184 | tf_op jit(solution)/shard_map/concatenate | solution.py:15
  (2 shorter events, 0.0 us)
Async XLA Ops:
  7.2 101.5 %copy-start = (bf16[512,2,128]{2,1,0:T(2,128)(2,1)S(1)}, bf16[512,2,128]{2,1,0:T(2,128)(2,1)}, u32[]{:S(2)}) copy-start(bf16[512,2,128]{2,1,0:T(2,128)(2,1)} %param.9) | copy-start | bytes 786436
  7.2 19.4 %copy-start.3 = (bf16[4,192,64]{1,2,0:T(8,128)(2,1)S(1)}, bf16[4,192,64]{1,2,0:T(8,128)(2,1)}, u32[]{:S(2)}) copy-start(bf16[4,192,64]{1,2,0:T(8,128)(2,1)} %param.6) | copy-start | bytes 294916
  7.2 23.4 %copy-start.2 = (bf16[512,2,128]{2,1,0:T(2,128)(2,1)S(1)}, bf16[512,2,128]{2,1,0:T(2,128)(2,1)}, u32[]{:S(2)}) copy-start(bf16[512,2,128]{2,1,0:T(2,128)(2,1)} %param.8) | copy-start | bytes 786436
  7.2 96.4 %all-gather.4.cloned.1.call-start = ((), (), s32[]{:S(2)}) async-start(), calls=%async_computation.2 | async-start | bytes 7077888 | tf_op jit(solution)/shard_map/all_gather | solution.py:42
  27.3 8.3 %all-to-all-start.1 = ((bf16[4,1,192,64]{2,3,1,0:T(8,128)(2,1)}), bf16[4,1,192,64]{2,3,1,0:T(8,128)(2,1)S(1)}, u32[]{:S(2)}, u32[]{:S(2)}) async-start(bf16[4,1,192,64]{2,3,1,0:T(8,128)(2,1)} %pad_maximum_fusion.1), calls=%async_computation.1 | async-start | bytes 262144 | tf_op jit(solution)/shard_map/all_to_all | solution.py:29
  108.2 2.8 %copy-start.1 = (bf16[4,1536,512]{2,1,0:T(8,128)(2,1)S(1)}, bf16[4,1536,512]{2,1,0:T(8,128)(2,1)}, u32[]{:S(2)}) copy-start(bf16[4,1536,512]{2,1,0:T(8,128)(2,1)} %all-gather.4.cloned.1.call-done) | copy-start | bytes 18874372
Sparse Core Ops, SparseCore 0:
  26.7 76.8 all-gather.3
